TPU v7x, 32 devices: a whole 2x2x4 slice. The times are simulated.
32 devices in a mesh: layer: 8 (over y, x, core), dp: 4 (over z).
Axes of the slice: x: 2, y: 2, z: 4, core: 2. Of those that a mesh axis runs over, the one named last changes fastest.
Arguments:
- weights: bfloat16 [32, 512, 512], P('layer', 'dp'), may hold values from -0.25 to 0.25
- biases: float32 [32, 512], P('layer'), may hold values from -3 to 3
- guesses: float32 [8, 2048, 512], P('layer', 'dp'), may hold values from -6 to 6
Outputs:
- states: bfloat16 [32, 2048, 512], P('layer', 'dp')
All inputs are finite; a program needn't handle non-finite values.
Results may differ from a plain program's by a relative error of at most 0.0041.
Values may be sent and summed in bfloat16 or wider, within the bound.
No kernel may reach another device: no remote copies, remote signals or barrier semaphores. Data moves between devices by JAX's collectives and lax.ppermute only.
A program may use at most 64 MiB of HBM per device.

v0:
```python
import jax
import jax.numpy as jnp
from jax import lax
from jax.sharding import PartitionSpec as P

GROUP = 4


def from_behind(value, axis, steps):
    count = lax.axis_size(axis)
    initial, last = (max(0, -steps), min(count, count - steps))
    return lax.ppermute(value, axis, [(source, source + steps) for source in range(initial, last)])


def advance(states_in, weight_mat, bias_row, step_width):
    preact = jnp.dot(states_in.astype(jnp.bfloat16), weight_mat, preferred_element_type=jnp.float32)
    return states_in + step_width * jnp.tanh(preact + bias_row)


def take_phase(rows_all, phase):
    grouped = rows_all.reshape(rows_all.shape[0] // GROUP, GROUP, rows_all.shape[1])
    return lax.dynamic_index_in_dim(grouped, phase, 1, keepdims=False)


def put_phase(rows_all, phase, values):
    grouped = rows_all.reshape(rows_all.shape[0] // GROUP, GROUP, rows_all.shape[1])
    grouped = lax.dynamic_update_index_in_dim(grouped, values, phase, 1)
    return grouped.reshape(rows_all.shape)


def per_device(weights, biases, guesses):
    layer_count = lax.axis_size("layer")
    layer_depth = weights.shape[0]
    layer_rank = lax.axis_index("layer")
    own_phase = layer_rank % GROUP
    leader_rank = layer_rank // GROUP
    leaders = layer_count // GROUP
    fine_width = 4.0 / (layer_depth * layer_count)
    block_width = layer_depth * fine_width
    group_width = GROUP * block_width
    full_weights = lax.all_gather(weights, "dp", axis=1, tiled=True)
    head_weight = full_weights[0]
    head_bias = biases[0]
    initial = guesses[0]

    def head_step(states_in, step_width):
        return advance(states_in, head_weight, head_bias, step_width)

    current = initial
    for layer_no in range(layer_depth):
        current = advance(current, full_weights[layer_no], biases[layer_no], fine_width)
    tau_one = from_behind(current - head_step(initial, block_width), "layer", 1)
    own_guess = take_phase(initial, own_phase)
    level = initial
    carried = head_step(own_guess, group_width)
    for member in range(1, GROUP + 1):
        outgoing = head_step(take_phase(level, (layer_rank + 1 - member) % GROUP), block_width)
        incoming, carried = from_behind((outgoing, carried), "layer", 1)
        landing = (layer_rank - member) % GROUP
        moved = incoming + take_phase(tau_one, landing)
        if member < GROUP:
            level = jnp.where(layer_rank >= 1, put_phase(level, landing, moved), level)
    tau_two = moved - carried
    coarse_state = jnp.where(layer_rank == 0, own_guess, moved)

    def leader_hop(turn_no, leader_state):
        arrived = from_behind(head_step(leader_state, group_width), "layer", GROUP)
        return jnp.where(leader_rank == turn_no, arrived + tau_two, leader_state)

    coarse_state = lax.fori_loop(1, leaders, leader_hop, coarse_state)
    corrected = put_phase(initial, own_phase, coarse_state)
    for member in range(1, GROUP):
        outgoing = head_step(take_phase(corrected, (layer_rank + 1 - member) % GROUP), block_width)
        incoming = from_behind(outgoing, "layer", 1)
        landing = (layer_rank - member) % GROUP
        renewed = incoming + take_phase(tau_one, landing)
        corrected = jnp.where(layer_rank >= 1, put_phase(corrected, landing, renewed), corrected)
    outputs = []
    current = corrected
    for layer_no in range(layer_depth):
        current = advance(current, full_weights[layer_no], biases[layer_no], fine_width)
        outputs.append(current.astype(jnp.bfloat16))
    return jnp.stack(outputs)


def solution(mesh):
    in_specs = (P("layer", "dp", None), P("layer", None), P("layer", "dp", None))
    out_specs = P("layer", "dp", None)
    return jax.shard_map(
        per_device, mesh=mesh, in_specs=in_specs, out_specs=out_specs, check_vma=False
    )
```

profile of v0, /device:TPU:4, one launch (start us, length us, event | category | flops | bytes accessed | tf_op | source)
XLA Modules:
  0.0 172.4 jit_solution(7225607612104073988)
XLA Ops:
  6.5 0.7 all-gather.2.cloned.1.call-update
  7.3 0.9 fusion.88
  8.1 47.7 %all-gather.2.cloned.1.call-done = bf16[4,512,512]{2,1,0:T(8,128)(2,1)} async-done(((bf16[4,128,512]{2,1,0:T(8,128)(2,1)}), bf16[4,512,512]{2,1,0:T(8,128)(2,1)}) %all-gather.2.cloned.1.call-update) | async-done | bytes 2097168 | tf_op jit(solution)/shard_map/all_gather | solution.py:41
  55.8 2.0 %fusion.22 = f32[512,512]{1,0:T(8,128)S(1)} fusion(f32[512]{0:T(512)S(1)} %bitcast.156, f32[1,512,512]{2,1,0:T(8,128)} %param.5, bf16[4,512,512]{2,1,0:T(8,128)(2,1)} %all-gather.2.cloned.1.call-done), kind=kOutput, calls=%fused_computation.31 | convolution fusion | flops 268959744 | bytes 2623488 | tf_op jit(solution)/shard_map/dot_general | solution.py:16
  57.8 0.1 copy-done
  57.9 0.6 fusion.21
  58.4 0.5 fusion.18
  58.9 1.5 fusion.15
  60.4 1.9 %collective-permute-start.1 = (f32[512,512]{1,0:T(8,128)}, f32[512,512]{1,0:T(8,128)}, u32[]{:S(2)}, u32[]{:S(2)}) collective-permute-start(f32[512,512]{1,0:T(8,128)} %fusion.15), channel_id=1, source_target_pairs={{0,4},{4,8},{8,12},{12,16},{16,20},{20,24},{24,28},{1,5},{5,9},{9,... | collective-permute-start | bytes 3145736 | tf_op jit(solution)/shard_map/ppermute | solution.py:12
  62.4 1.3 reshape_squeeze.2
  63.6 1.6 fusion.87
  65.3 0.7 copy-done.8
  66.0 1.1 bitcast_add_fusion.3
  67.0 3.5 %collective-permute-start = (f32[128,512]{1,0:T(8,128)}, f32[128,512]{1,0:T(8,128)}, u32[]{:S(2)}, u32[]{:S(2)}) collective-permute-start(f32[128,512]{1,0:T(8,128)} %get-tuple-element.33), channel_id=1, source_target_pairs={{0,4},{4,8},{8,12},{12,16},{16,20},{20,24},{24,28},{1,5},{5,9},{9,... | collective-permute-start | bytes 786440 | tf_op jit(solution)/shard_map/ppermute | solution.py:12
  70.6 1.3 copy.23
  71.9 1.2 copy.78
  73.1 1.9 %collective-permute-start.6 = (f32[128,512]{1,0:T(8,128)}, f32[128,512]{1,0:T(8,128)}, u32[]{:S(2)}, u32[]{:S(2)}) collective-permute-start(f32[128,512]{1,0:T(8,128)} %get-tuple-element.32), channel_id=1, source_target_pairs={{0,4},{4,8},{8,12},{12,16},{16,20},{20,24},{24,28},{1,5},{5,9},{9,... | collective-permute-start | bytes 786440 | tf_op jit(solution)/shard_map/ppermute | solution.py:12
  75.0 2.7 %collective-permute-done.1 = f32[512,512]{1,0:T(8,128)} collective-permute-done((f32[512,512]{1,0:T(8,128)}, f32[512,512]{1,0:T(8,128)}, u32[]{:S(2)}, u32[]{:S(2)}) %collective-permute-start.1) | collective-permute-done | bytes 1048608 | tf_op jit(solution)/shard_map/ppermute | solution.py:12
  77.7 2.5 %reshape.21 = f32[128,4,512]{2,1,0:T(4,128)} reshape(f32[512,512]{1,0:T(8,128)} %collective-permute-done.1) | data formatting | bytes 2097152 | tf_op jit(solution)/shard_map/reshape | solution.py:21
  80.2 4.2 %constant_dynamic-slice_fusion = (f32[128,1,512]{2,1,0:T(1,128)}, f32[128,1,512]{2,1,0:T(1,128)S(1)}, f32[128,1,512]{2,1,0:T(1,128)S(1)}, f32[128,1,512]{2,1,0:T(1,128)S(1)}) fusion(f32[128,4,512]{2,1,0:T(4,128)} %reshape.21, s32[]{:T(128)S(6)} %select_n.179, s32[]{:T(128)S(6)} %select_n.174, s32[]{:T(128)S(6)} %select_n.169, s32[]{:T(128)S(6)} %select_n.164), kind=kLoop, calls=%fused_computation.121 | loop fusion | bytes 2097168 | tf_op jit(solution)/shard_map/jit(dynamic_index_in_dim)/dynamic_slice | solution.py:22
  84.5 1.2 fusion.59
  85.7 0.2 fusion.46
  85.9 1.9 %collective-permute-start.2 = (f32[128,512]{1,0:T(8,128)S(1)}, f32[128,512]{1,0:T(8,128)S(1)}, u32[]{:S(2)}, u32[]{:S(2)}) collective-permute-start(f32[128,512]{1,0:T(8,128)S(1)} %fusion.46), channel_id=1, source_target_pairs={{0,4},{4,8},{8,12},{12,16},{16,20},{20,24},{24,28},{1,5},{5,9},{9,... | collective-permute-start | bytes 786440 | tf_op jit(solution)/shard_map/ppermute | solution.py:12
  87.9 2.6 %collective-permute-start.7 = (f32[128,512]{1,0:T(8,128)}, f32[128,512]{1,0:T(8,128)}, u32[]{:S(2)}, u32[]{:S(2)}) collective-permute-start(f32[128,512]{1,0:T(8,128)} %collective-permute-done.6), channel_id=1, source_target_pairs={{0,4},{4,8},{8,12},{12,16},{16,20},{20,24},{24,28},{1,5},{5,9},{9,... | collective-permute-start | bytes 786440 | tf_op jit(solution)/shard_map/ppermute | solution.py:12
  90.5 4.1 %collective-permute-done.2 = f32[128,512]{1,0:T(8,128)S(1)} collective-permute-done((f32[128,512]{1,0:T(8,128)S(1)}, f32[128,512]{1,0:T(8,128)S(1)}, u32[]{:S(2)}, u32[]{:S(2)}) %collective-permute-start.2) | collective-permute-done | bytes 262176 | tf_op jit(solution)/shard_map/ppermute | solution.py:12
  94.5 0.1 fusion.58
  94.6 0.2 fusion.45
  94.9 1.9 %collective-permute-start.3 = (f32[128,512]{1,0:T(8,128)S(1)}, f32[128,512]{1,0:T(8,128)S(1)}, u32[]{:S(2)}, u32[]{:S(2)}) collective-permute-start(f32[128,512]{1,0:T(8,128)S(1)} %fusion.45), channel_id=1, source_target_pairs={{0,4},{4,8},{8,12},{12,16},{16,20},{20,24},{24,28},{1,5},{5,9},{9,... | collective-permute-start | bytes 786440 | tf_op jit(solution)/shard_map/ppermute | solution.py:12
  96.8 0.6 collective-permute-done.7
  97.4 1.9 %collective-permute-start.8 = (f32[128,512]{1,0:T(8,128)}, f32[128,512]{1,0:T(8,128)}, u32[]{:S(2)}, u32[]{:S(2)}) collective-permute-start(f32[128,512]{1,0:T(8,128)} %collective-permute-done.7), channel_id=1, source_target_pairs={{0,4},{4,8},{8,12},{12,16},{16,20},{20,24},{24,28},{1,5},{5,9},{9,... | collective-permute-start | bytes 786440 | tf_op jit(solution)/shard_map/ppermute | solution.py:12
  99.4 4.1 %collective-permute-done.3 = f32[128,512]{1,0:T(8,128)S(1)} collective-permute-done((f32[128,512]{1,0:T(8,128)S(1)}, f32[128,512]{1,0:T(8,128)S(1)}, u32[]{:S(2)}, u32[]{:S(2)}) %collective-permute-start.3) | collective-permute-done | bytes 262176 | tf_op jit(solution)/shard_map/ppermute | solution.py:12
  103.5 0.1 fusion.57
  103.6 1.0 fusion.44
  104.5 1.9 %collective-permute-start.4 = (f32[128,512]{1,0:T(8,128)}, f32[128,512]{1,0:T(8,128)}, u32[]{:S(2)}, u32[]{:S(2)}) collective-permute-start(f32[128,512]{1,0:T(8,128)} %fusion.44), channel_id=1, source_target_pairs={{0,4},{4,8},{8,12},{12,16},{16,20},{20,24},{24,28},{1,5},{5,9},{9,... | collective-permute-start | bytes 786440 | tf_op jit(solution)/shard_map/ppermute | solution.py:12
  106.5 1.9 %collective-permute-start.9 = (f32[128,512]{1,0:T(8,128)}, f32[128,512]{1,0:T(8,128)}, u32[]{:S(2)}, u32[]{:S(2)}) collective-permute-start(f32[128,512]{1,0:T(8,128)} %collective-permute-done.8), channel_id=1, source_target_pairs={{0,4},{4,8},{8,12},{12,16},{16,20},{20,24},{24,28},{1,5},{5,9},{9,... | collective-permute-start | bytes 786440 | tf_op jit(solution)/shard_map/ppermute | solution.py:12
  108.4 5.0 %collective-permute-done.4 = f32[128,512]{1,0:T(8,128)} collective-permute-done((f32[128,512]{1,0:T(8,128)}, f32[128,512]{1,0:T(8,128)}, u32[]{:S(2)}, u32[]{:S(2)}) %collective-permute-start.4) | collective-permute-done | bytes 262176 | tf_op jit(solution)/shard_map/ppermute | solution.py:12
  113.4 2.3 %fusion.43 = f32[128,512]{1,0:T(8,128)} fusion(f32[128,1,512]{2,1,0:T(1,128)} %copy-done.8, f32[512]{0:T(512)S(1)} %bitcast.161, pred[]{:T(512)S(6)} %eq.24, f32[128,512]{1,0:T(8,128)} %collective-permute-done.4, f32[128,1,512]{2,1,0:T(1,128)} %get-tuple-element.19, bf16[4,512,512]{2,1,0:T(8,128)(2,1)S(1)} %copy-done), kind=kOutput, calls=%fused_computation.60 | convolution fusion | flops 67633152 | bytes 2362368 | tf_op jit(solution)/shard_map/while/body/eval_jaxpr/dot_general | solution.py:16
  115.8 1.3 collective-permute-start.5
  117.1 7.2 %collective-permute-done.5 = f32[128,512]{1,0:T(8,128)} collective-permute-done((f32[128,512]{1,0:T(8,128)}, f32[128,512]{1,0:T(8,128)}, u32[]{:S(2)}, u32[]{:S(2)}) %collective-permute-start.5) | collective-permute-done | bytes 262176 | tf_op jit(solution)/shard_map/while/body/eval_jaxpr/ppermute | solution.py:12
  124.3 1.4 bitcast_dynamic-update-slice_fusion
  125.7 0.2 fusion.42
  126.0 1.9 %collective-permute-start.10 = (f32[128,512]{1,0:T(8,128)S(1)}, f32[128,512]{1,0:T(8,128)S(1)}, u32[]{:S(2)}, u32[]{:S(2)}) collective-permute-start(f32[128,512]{1,0:T(8,128)S(1)} %fusion.42), channel_id=1, source_target_pairs={{0,4},{4,8},{8,12},{12,16},{16,20},{20,24},{24,28},{1,5},{5,9},{9,... | collective-permute-start | bytes 786440 | tf_op jit(solution)/shard_map/ppermute | solution.py:12
  127.9 6.7 %collective-permute-done.10 = f32[128,512]{1,0:T(8,128)S(1)} collective-permute-done((f32[128,512]{1,0:T(8,128)S(1)}, f32[128,512]{1,0:T(8,128)S(1)}, u32[]{:S(2)}, u32[]{:S(2)}) %collective-permute-start.10) | collective-permute-done | bytes 262176 | tf_op jit(solution)/shard_map/ppermute | solution.py:12
  134.6 0.1 fusion.56
  134.7 0.2 fusion.41
  134.9 1.9 %collective-permute-start.11 = (f32[128,512]{1,0:T(8,128)S(1)}, f32[128,512]{1,0:T(8,128)S(1)}, u32[]{:S(2)}, u32[]{:S(2)}) collective-permute-start(f32[128,512]{1,0:T(8,128)S(1)} %fusion.41), channel_id=1, source_target_pairs={{0,4},{4,8},{8,12},{12,16},{16,20},{20,24},{24,28},{1,5},{5,9},{9,... | collective-permute-start | bytes 786440 | tf_op jit(solution)/shard_map/ppermute | solution.py:12
  136.8 6.7 %collective-permute-done.11 = f32[128,512]{1,0:T(8,128)S(1)} collective-permute-done((f32[128,512]{1,0:T(8,128)S(1)}, f32[128,512]{1,0:T(8,128)S(1)}, u32[]{:S(2)}, u32[]{:S(2)}) %collective-permute-start.11) | collective-permute-done | bytes 262176 | tf_op jit(solution)/shard_map/ppermute | solution.py:12
  143.5 0.1 fusion.55
  143.6 0.2 fusion.40
  143.8 1.9 %collective-permute-start.12 = (f32[128,512]{1,0:T(8,128)S(1)}, f32[128,512]{1,0:T(8,128)S(1)}, u32[]{:S(2)}, u32[]{:S(2)}) collective-permute-start(f32[128,512]{1,0:T(8,128)S(1)} %fusion.40), channel_id=1, source_target_pairs={{0,4},{4,8},{8,12},{12,16},{16,20},{20,24},{24,28},{1,5},{5,9},{9,... | collective-permute-start | bytes 786440 | tf_op jit(solution)/shard_map/ppermute | solution.py:12
  145.8 6.7 %collective-permute-done.12 = f32[128,512]{1,0:T(8,128)S(1)} collective-permute-done((f32[128,512]{1,0:T(8,128)S(1)}, f32[128,512]{1,0:T(8,128)S(1)}, u32[]{:S(2)}, u32[]{:S(2)}) %collective-permute-start.12) | collective-permute-done | bytes 262176 | tf_op jit(solution)/shard_map/ppermute | solution.py:12
  152.4 0.1 fusion.54
  152.5 1.6 copy.24
  154.2 0.9 convert_element_type.105
  155.0 1.6 select_n.185
  156.6 2.2 %copy.25 = bf16[128,4,512]{2,1,0:T(4,128)(2,1)} copy(bf16[128,4,512]{2,0,1:T(8,128)(2,1)} %convert_element_type.105) | data formatting | bytes 1048576 | tf_op jit(solution)/shard_map/convert_element_type | solution.py:16
  158.9 2.0 %convert_element_type.106 = bf16[512,512]{1,0:T(8,128)(2,1)} reshape(bf16[128,4,512]{2,1,0:T(4,128)(2,1)} %copy.25) | data formatting | bytes 1048576 | tf_op jit(solution)/shard_map/convert_element_type | solution.py:16
  160.8 1.5 fusion.11
  162.3 0.1 convert_bitcast_fusion.2
  162.4 0.4 fusion.8
  162.9 0.5 fusion.5
  163.3 0.1 convert_bitcast_fusion
  163.5 0.5 fusion.24
  164.0 1.6 pad_maximum_fusion
  (21 shorter events, 0.0 us)
Async XLA Ops:
  6.5 51.2 %copy-start.2 = (f32[1,512,512]{2,1,0:T(8,128)S(1)}, f32[1,512,512]{2,1,0:T(8,128)}, u32[]{:S(2)}) copy-start(f32[1,512,512]{2,1,0:T(8,128)} %param.5) | copy-start | bytes 3145732
  6.5 49.3 %all-gather.2.cloned.1.call-start = ((), (), s32[]{:S(2)}) async-start(), calls=%async_computation | async-start | bytes 2621440 | tf_op jit(solution)/shard_map/all_gather | solution.py:41
  55.8 2.1 %copy-start = (bf16[4,512,512]{2,1,0:T(8,128)(2,1)S(1)}, bf16[4,512,512]{2,1,0:T(8,128)(2,1)}, u32[]{:S(2)}) copy-start(bf16[4,512,512]{2,1,0:T(8,128)(2,1)} %all-gather.2.cloned.1.call-done) | copy-start | bytes 6291460
  60.4 17.3 %collective-permute-start.1 = (f32[512,512]{1,0:T(8,128)}, f32[512,512]{1,0:T(8,128)}, u32[]{:S(2)}, u32[]{:S(2)}) collective-permute-start(f32[512,512]{1,0:T(8,128)} %fusion.15), channel_id=1, source_target_pairs={{0,4},{4,8},{8,12},{12,16},{16,20},{20,24},{24,28},{1,5},{5,9},{9,... | collective-permute-start | bytes 3145736 | tf_op jit(solution)/shard_map/ppermute | solution.py:12
  63.6 6.9 %copy-start.3 = (f32[128,4,512]{2,1,0:T(4,128)S(1)}, f32[128,4,512]{2,1,0:T(4,128)}, u32[]{:S(2)}) copy-start(f32[128,4,512]{2,1,0:T(4,128)} %reshape_squeeze.2) | copy-start | bytes 3145732
  65.3 0.7 copy-start.8
  67.0 17.4 %collective-permute-start = (f32[128,512]{1,0:T(8,128)}, f32[128,512]{1,0:T(8,128)}, u32[]{:S(2)}, u32[]{:S(2)}) collective-permute-start(f32[128,512]{1,0:T(8,128)} %get-tuple-element.33), channel_id=1, source_target_pairs={{0,4},{4,8},{8,12},{12,16},{16,20},{20,24},{24,28},{1,5},{5,9},{9,... | collective-permute-start | bytes 786440 | tf_op jit(solution)/shard_map/ppermute | solution.py:12
  73.1 14.8 %collective-permute-start.6 = (f32[128,512]{1,0:T(8,128)}, f32[128,512]{1,0:T(8,128)}, u32[]{:S(2)}, u32[]{:S(2)}) collective-permute-start(f32[128,512]{1,0:T(8,128)} %get-tuple-element.32), channel_id=1, source_target_pairs={{0,4},{4,8},{8,12},{12,16},{16,20},{20,24},{24,28},{1,5},{5,9},{9,... | collective-permute-start | bytes 786440 | tf_op jit(solution)/shard_map/ppermute | solution.py:12
  80.2 4.2 %copy-start.1 = (f32[128,4,512]{2,0,1:T(8,128)S(1)}, f32[128,4,512]{2,0,1:T(8,128)}, u32[]{:S(2)}) copy-start(f32[128,4,512]{2,0,1:T(8,128)} %copy.23) | copy-start | bytes 3145732
  84.4 10.4 %copy-start.4 = (f32[128,1,512]{2,1,0:T(1,128)}, f32[128,1,512]{2,1,0:T(1,128)S(1)}, u32[]{:S(2)}) copy-start(f32[128,1,512]{2,1,0:T(1,128)S(1)} %get-tuple-element.28) | copy-start | bytes 786436
  84.4 10.4 %copy-start.6 = (f32[128,1,512]{2,1,0:T(1,128)}, f32[128,1,512]{2,1,0:T(1,128)S(1)}, u32[]{:S(2)}) copy-start(f32[128,1,512]{2,1,0:T(1,128)S(1)} %get-tuple-element.30) | copy-start | bytes 786436
  85.9 8.6 %collective-permute-start.2 = (f32[128,512]{1,0:T(8,128)S(1)}, f32[128,512]{1,0:T(8,128)S(1)}, u32[]{:S(2)}, u32[]{:S(2)}) collective-permute-start(f32[128,512]{1,0:T(8,128)S(1)} %fusion.46), channel_id=1, source_target_pairs={{0,4},{4,8},{8,12},{12,16},{16,20},{20,24},{24,28},{1,5},{5,9},{9,... | collective-permute-start | bytes 786440 | tf_op jit(solution)/shard_map/ppermute | solution.py:12
  87.9 9.6 %collective-permute-start.7 = (f32[128,512]{1,0:T(8,128)}, f32[128,512]{1,0:T(8,128)}, u32[]{:S(2)}, u32[]{:S(2)}) collective-permute-start(f32[128,512]{1,0:T(8,128)} %collective-permute-done.6), channel_id=1, source_target_pairs={{0,4},{4,8},{8,12},{12,16},{16,20},{20,24},{24,28},{1,5},{5,9},{9,... | collective-permute-start | bytes 786440 | tf_op jit(solution)/shard_map/ppermute | solution.py:12
  94.9 8.6 %collective-permute-start.3 = (f32[128,512]{1,0:T(8,128)S(1)}, f32[128,512]{1,0:T(8,128)S(1)}, u32[]{:S(2)}, u32[]{:S(2)}) collective-permute-start(f32[128,512]{1,0:T(8,128)S(1)} %fusion.45), channel_id=1, source_target_pairs={{0,4},{4,8},{8,12},{12,16},{16,20},{20,24},{24,28},{1,5},{5,9},{9,... | collective-permute-start | bytes 786440 | tf_op jit(solution)/shard_map/ppermute | solution.py:12
  97.4 9.0 %collective-permute-start.8 = (f32[128,512]{1,0:T(8,128)}, f32[128,512]{1,0:T(8,128)}, u32[]{:S(2)}, u32[]{:S(2)}) collective-permute-start(f32[128,512]{1,0:T(8,128)} %collective-permute-done.7), channel_id=1, source_target_pairs={{0,4},{4,8},{8,12},{12,16},{16,20},{20,24},{24,28},{1,5},{5,9},{9,... | collective-permute-start | bytes 786440 | tf_op jit(solution)/shard_map/ppermute | solution.py:12
  104.5 8.9 %collective-permute-start.4 = (f32[128,512]{1,0:T(8,128)}, f32[128,512]{1,0:T(8,128)}, u32[]{:S(2)}, u32[]{:S(2)}) collective-permute-start(f32[128,512]{1,0:T(8,128)} %fusion.44), channel_id=1, source_target_pairs={{0,4},{4,8},{8,12},{12,16},{16,20},{20,24},{24,28},{1,5},{5,9},{9,... | collective-permute-start | bytes 786440 | tf_op jit(solution)/shard_map/ppermute | solution.py:12
  106.5 10.6 %collective-permute-start.9 = (f32[128,512]{1,0:T(8,128)}, f32[128,512]{1,0:T(8,128)}, u32[]{:S(2)}, u32[]{:S(2)}) collective-permute-start(f32[128,512]{1,0:T(8,128)} %collective-permute-done.8), channel_id=1, source_target_pairs={{0,4},{4,8},{8,12},{12,16},{16,20},{20,24},{24,28},{1,5},{5,9},{9,... | collective-permute-start | bytes 786440 | tf_op jit(solution)/shard_map/ppermute | solution.py:12
  115.8 8.6 %collective-permute-start.5 = (f32[128,512]{1,0:T(8,128)}, f32[128,512]{1,0:T(8,128)}, u32[]{:S(2)}, u32[]{:S(2)}) collective-permute-start(f32[128,512]{1,0:T(8,128)} %fusion.43), channel_id=1, source_target_pairs={{0,16},{4,20},{8,24},{12,28},{1,17},{5,21},{9,25},{13,29},{2,18},{... | collective-permute-start | bytes 786440 | tf_op jit(solution)/shard_map/while/body/eval_jaxpr/ppermute | solution.py:12
  117.1 17.5 %copy-start.7 = (f32[128,1,512]{2,1,0:T(1,128)S(1)}, f32[128,1,512]{2,1,0:T(1,128)}, u32[]{:S(2)}) copy-start(f32[128,1,512]{2,1,0:T(1,128)} %copy-done.6) | copy-start | bytes 786436
  125.7 17.8 %copy-start.5 = (f32[128,1,512]{2,1,0:T(1,128)S(1)}, f32[128,1,512]{2,1,0:T(1,128)}, u32[]{:S(2)}) copy-start(f32[128,1,512]{2,1,0:T(1,128)} %copy-done.4) | copy-start | bytes 786436
  126.0 8.6 %collective-permute-start.10 = (f32[128,512]{1,0:T(8,128)S(1)}, f32[128,512]{1,0:T(8,128)S(1)}, u32[]{:S(2)}, u32[]{:S(2)}) collective-permute-start(f32[128,512]{1,0:T(8,128)S(1)} %fusion.42), channel_id=1, source_target_pairs={{0,4},{4,8},{8,12},{12,16},{16,20},{20,24},{24,28},{1,5},{5,9},{9,... | collective-permute-start | bytes 786440 | tf_op jit(solution)/shard_map/ppermute | solution.py:12
  134.9 8.6 %collective-permute-start.11 = (f32[128,512]{1,0:T(8,128)S(1)}, f32[128,512]{1,0:T(8,128)S(1)}, u32[]{:S(2)}, u32[]{:S(2)}) collective-permute-start(f32[128,512]{1,0:T(8,128)S(1)} %fusion.41), channel_id=1, source_target_pairs={{0,4},{4,8},{8,12},{12,16},{16,20},{20,24},{24,28},{1,5},{5,9},{9,... | collective-permute-start | bytes 786440 | tf_op jit(solution)/shard_map/ppermute | solution.py:12
  143.8 8.6 %collective-permute-start.12 = (f32[128,512]{1,0:T(8,128)S(1)}, f32[128,512]{1,0:T(8,128)S(1)}, u32[]{:S(2)}, u32[]{:S(2)}) collective-permute-start(f32[128,512]{1,0:T(8,128)S(1)} %fusion.40), channel_id=1, source_target_pairs={{0,4},{4,8},{8,12},{12,16},{16,20},{20,24},{24,28},{1,5},{5,9},{9,... | collective-permute-start | bytes 786440 | tf_op jit(solution)/shard_map/ppermute | solution.py:12
Sparse Core Ops, SparseCore 0:
  8.9 46.8 all-gather.1
where the time goes:
time: 173 us; the launch traced here: 172 us
  waiting for transfers between devices  92.2 us (53%)
  starting transfers between devices  26.5 us (15%)
  local copies, waits for them, and re-layouts  19.6 us (11%)
  between operations  13.9 us (8%)
  matrix products  12.9 us (7%)
  other arithmetic  7.32 us (4%)
    all_gather x1, waiting for transfers between devices, per_device(): full_weights = lax.all_gather(weights, 'dp', axis=1, tiled=True)  47.7 us
    ppermute x13, waiting for transfers between devices, from_behind(): lax.ppermute(value, axis, [(source, source + steps) for source in range(i...  43.8 us
    ppermute x13, starting transfers between devices, from_behind(): lax.ppermute(value, axis, [(source, source + steps) for source in range(i...  26.5 us
    dot_general x16, matrix products, advance(): jnp.dot(states_in.astype(jnp.bfloat16), weight_mat, preferred_element_typ...  12.9 us
    convert_element_type x2, local copies, waits for them, and re-layouts, advance(): states_in.astype(jnp.bfloat16)  4.21 us
    dynamic_slice x1, local copies, waits for them, and re-layouts, take_phase(): return lax.dynamic_index_in_dim(grouped, phase, 1, keepdims=False)  4.21 us
  transfers between devices with their start and end apart: 14, of which 10 were waited for; matrix products, arithmetic and copies ran while one was open for 11% of the time, Pallas kernels for 0%

commit v1 on v0

--- a/solution.py
+++ b/solution.py
@@ -38,7 +38,12 @@
     fine_width = 4.0 / (layer_depth * layer_count)
     block_width = layer_depth * fine_width
     group_width = GROUP * block_width
-    full_weights = lax.all_gather(weights, "dp", axis=1, tiled=True)
+    ring = [weights]
+    for hop in range(3):
+        ring.append(lax.ppermute(ring[-1], "dp", [(dev, (dev + 1) % 4) for dev in range(4)]))
+    full_weights = jnp.roll(
+        jnp.concatenate(ring[::-1], axis=1), (lax.axis_index("dp") + 1) * ring[0].shape[1], axis=1
+    )
     head_weight = full_weights[0]
     head_bias = biases[0]
     initial = guesses[0]

time: 173 us -> 160 us (0.925)
  between operations: 13.9 us -> 0.67 us
  matrix products: 12.9 us -> 19.7 us
  waiting for transfers between devices: 92.2 us -> 87.4 us
  other arithmetic: 7.32 us -> 3.48 us
  starting transfers between devices: 26.5 us -> 28.6 us
    all_gather x1 -> x0, waiting for transfers between devices: 47.7 us -> none  [per_device(): full_weights = lax.all_gather(weights, 'dp', axis=1, tiled=True)]
    ppermute x0 -> x3, waiting for transfers between devices: none -> 40.8 us  [per_device(): lax.ppermute(ring[-1], 'dp', [(dev, (dev + 1) % 4) for dev in range(4)])]
    dot_general x16, matrix products: 12.9 us -> 19.7 us  [advance(): jnp.dot(states_in.astype(jnp.bfloat16), weight_mat, preferred_element_typ...]
    unnamed x19 -> x29, local copies, waits for them, and re-layouts: 2.03 us -> 6.31 us
    ppermute x13, waiting for transfers between devices: 43.8 us -> 46.5 us  [from_behind(): lax.ppermute(value, axis, [(source, source + steps) for source in range(i...]
    convert_element_type x2, local copies, waits for them, and re-layouts: 4.21 us -> 1.58 us  [advance(): states_in.astype(jnp.bfloat16)]
    dynamic_slice x1, local copies, waits for them, and re-layouts: 4.21 us -> 1.61 us  [take_phase(): return lax.dynamic_index_in_dim(grouped, phase, 1, keepdims=False)]
    ppermute x0 -> x1, local copies, waits for them, and re-layouts: none -> 2.53 us  [from_behind(): lax.ppermute(value, axis, [(source, source + steps) for source in range(i...]
  transfers between devices with their start and end apart: 14 -> 16, of which waited for: 10 -> 12; matrix products, arithmetic and copies ran while one was open for 11% -> 11% of each run, Pallas kernels for 0% -> 0%
where the time goes in v1:
time: 160 us; the launch traced here: 159 us
  waiting for transfers between devices  87.4 us (55%)
  starting transfers between devices  28.6 us (18%)
  matrix products  19.7 us (12%)
  local copies, waits for them, and re-layouts  18.8 us (12%)
  other arithmetic  3.48 us (2%)
    ppermute x13, waiting for transfers between devices, from_behind(): lax.ppermute(value, axis, [(source, source + steps) for source in range(i...  46.5 us
    ppermute x3, waiting for transfers between devices, per_device(): lax.ppermute(ring[-1], 'dp', [(dev, (dev + 1) % 4) for dev in range(4)])  40.8 us
    ppermute x13, starting transfers between devices, from_behind(): lax.ppermute(value, axis, [(source, source + steps) for source in range(i...  27 us
    dot_general x16, matrix products, advance(): jnp.dot(states_in.astype(jnp.bfloat16), weight_mat, preferred_element_typ...  19.7 us
    unnamed x29, local copies, waits for them, and re-layouts  6.31 us
  transfers between devices with their start and end apart: 16, of which 12 were waited for; matrix products, arithmetic and copies ran while one was open for 11% of the time, Pallas kernels for 0%

profile of v1, /device:TPU:4, one launch (start us, length us, event | category | flops | bytes accessed | tf_op | source)
XLA Modules:
  0.0 158.7 jit_solution(5620941228953129687)
XLA Ops:
  0.0 1.6 collective-permute-start
  1.6 14.2 %collective-permute-done = bf16[4,128,512]{2,1,0:T(8,128)(2,1)S(1)} collective-permute-done((bf16[4,128,512]{2,1,0:T(8,128)(2,1)}, bf16[4,128,512]{2,1,0:T(8,128)(2,1)S(1)}, u32[]{:S(2)}, u32[]{:S(2)}) %collective-permute-start) | collective-permute-done | bytes 524320 | tf_op jit(solution)/shard_map/ppermute | solution.py:43
  15.8 14.8 %collective-permute-done.1 = bf16[4,128,512]{2,1,0:T(8,128)(2,1)} collective-permute-done((bf16[4,128,512]{2,1,0:T(8,128)(2,1)S(1)}, bf16[4,128,512]{2,1,0:T(8,128)(2,1)}, u32[]{:S(2)}, u32[]{:S(2)}) %collective-permute-start.1) | collective-permute-done | bytes 524320 | tf_op jit(solution)/shard_map/ppermute | solution.py:43
  30.7 1.6 copy.35
  32.2 0.9 fusion.103
  33.1 11.8 %collective-permute-done.2 = bf16[4,128,512]{2,1,0:T(8,128)(2,1)} collective-permute-done((bf16[4,128,512]{2,1,0:T(8,128)(2,1)}, bf16[4,128,512]{2,1,0:T(8,128)(2,1)}, u32[]{:S(2)}, u32[]{:S(2)}) %collective-permute-start.2) | collective-permute-done | bytes 524320 | tf_op jit(solution)/shard_map/ppermute | solution.py:43
  44.8 1.1 constant_dynamic-update-slice_fusion.7
  45.9 1.1 constant_dynamic-update-slice_fusion.6
  47.1 1.1 constant_dynamic-update-slice_fusion.3
  48.2 1.1 constant_dynamic-update-slice_fusion.2
  49.4 0.5 fusion.22
  49.9 0.6 fusion.21
  50.5 0.5 fusion.18
  51.1 0.2 copy-done
  51.3 0.6 fusion.15
  52.0 1.9 %collective-permute-start.4 = (f32[512,512]{0,1:T(8,128)S(1)}, f32[512,512]{0,1:T(8,128)}, u32[]{:S(2)}, u32[]{:S(2)}) collective-permute-start(f32[512,512]{0,1:T(8,128)S(1)} %fusion.15), channel_id=1, source_target_pairs={{0,4},{4,8},{8,12},{12,16},{16,20},{20,24},{24,28},{1,5},{5,9},{9,... | collective-permute-start | bytes 3145736 | tf_op jit(solution)/shard_map/ppermute | solution.py:12
  53.9 0.3 reshape_squeeze.2
  54.2 0.3 fusion.102
  54.6 2.1 %bitcast_add_fusion.10 = (f32[128,512]{1,0:T(8,128)}, f32[128,512]{1,0:T(8,128)}) fusion(f32[128,1,512]{2,1,0:T(1,128)S(1)} %get-tuple-element.18, f32[512]{0:T(512)S(1)} %bitcast.204, bf16[4,1024,512]{2,1,0:T(8,128)(2,1)} %copy-done, s32[]{:T(128)S(6)} %select_n.176, bf16[128,1,512]{2,1,0:T(2,128)(2,1)S(1)} %get-tuple-element.17), kind=kOutput, calls=%fused_computation.100 | convolution fusion | flops 67436544 | bytes 1443844 | tf_op jit(solution)/shard_map/dot_general | solution.py:16
  56.7 3.5 %collective-permute-start.3 = (f32[128,512]{1,0:T(8,128)}, f32[128,512]{1,0:T(8,128)}, u32[]{:S(2)}, u32[]{:S(2)}) collective-permute-start(f32[128,512]{1,0:T(8,128)} %get-tuple-element.33), channel_id=1, source_target_pairs={{0,4},{4,8},{8,12},{12,16},{16,20},{20,24},{24,28},{1,5},{5,9},{9,... | collective-permute-start | bytes 786440 | tf_op jit(solution)/shard_map/ppermute | solution.py:12
  60.3 0.3 copy.43
  60.7 1.9 %collective-permute-start.9 = (f32[128,512]{1,0:T(8,128)}, f32[128,512]{1,0:T(8,128)}, u32[]{:S(2)}, u32[]{:S(2)}) collective-permute-start(f32[128,512]{1,0:T(8,128)} %get-tuple-element.32), channel_id=1, source_target_pairs={{0,4},{4,8},{8,12},{12,16},{16,20},{20,24},{24,28},{1,5},{5,9},{9,... | collective-permute-start | bytes 786440 | tf_op jit(solution)/shard_map/ppermute | solution.py:12
  62.6 6.5 %collective-permute-done.4 = f32[512,512]{0,1:T(8,128)} collective-permute-done((f32[512,512]{0,1:T(8,128)S(1)}, f32[512,512]{0,1:T(8,128)}, u32[]{:S(2)}, u32[]{:S(2)}) %collective-permute-start.4) | collective-permute-done | bytes 1048608 | tf_op jit(solution)/shard_map/ppermute | solution.py:12
  69.1 2.5 %copy.40 = f32[512,512]{1,0:T(8,128)} copy(f32[512,512]{0,1:T(8,128)} %collective-permute-done.4) | data formatting | bytes 2097152 | tf_op jit(solution)/shard_map/ppermute | solution.py:12
  71.6 1.5 reshape.21
  73.1 1.6 %constant_dynamic-slice_fusion = (f32[128,1,512]{2,1,0:T(1,128)}, f32[128,1,512]{2,1,0:T(1,128)S(1)}, f32[128,1,512]{2,1,0:T(1,128)S(1)}, f32[128,1,512]{2,1,0:T(1,128)S(1)}) fusion(f32[128,4,512]{2,1,0:T(4,128)S(1)} %reshape.21, s32[]{:T(128)S(6)} %select_n.193, s32[]{:T(128)S(6)} %select_n.188, s32[]{:T(128)S(6)} %select_n.183, s32[]{:T(128)S(6)} %select_n.178), kind=kLoop, calls=%fused_computation.141 | loop fusion | bytes 2097168 | tf_op jit(solution)/shard_map/jit(dynamic_index_in_dim)/dynamic_slice | solution.py:22
  74.8 1.3 fusion.66
  76.1 1.3 fusion.46
  77.4 1.9 %collective-permute-start.5 = (f32[128,512]{1,0:T(8,128)S(1)}, f32[128,512]{1,0:T(8,128)S(1)}, u32[]{:S(2)}, u32[]{:S(2)}) collective-permute-start(f32[128,512]{1,0:T(8,128)S(1)} %fusion.46), channel_id=1, source_target_pairs={{0,4},{4,8},{8,12},{12,16},{16,20},{20,24},{24,28},{1,5},{5,9},{9,... | collective-permute-start | bytes 786440 | tf_op jit(solution)/shard_map/ppermute | solution.py:12
  79.3 2.6 %collective-permute-start.10 = (f32[128,512]{1,0:T(8,128)}, f32[128,512]{1,0:T(8,128)S(1)}, u32[]{:S(2)}, u32[]{:S(2)}) collective-permute-start(f32[128,512]{1,0:T(8,128)} %collective-permute-done.9), channel_id=1, source_target_pairs={{0,4},{4,8},{8,12},{12,16},{16,20},{20,24},{24,28},{1,5},{5,9},{9,... | collective-permute-start | bytes 786440 | tf_op jit(solution)/shard_map/ppermute | solution.py:12
  81.9 4.0 %collective-permute-done.5 = f32[128,512]{1,0:T(8,128)S(1)} collective-permute-done((f32[128,512]{1,0:T(8,128)S(1)}, f32[128,512]{1,0:T(8,128)S(1)}, u32[]{:S(2)}, u32[]{:S(2)}) %collective-permute-start.5) | collective-permute-done | bytes 262176 | tf_op jit(solution)/shard_map/ppermute | solution.py:12
  86.1 1.3 fusion.45
  87.4 1.9 %collective-permute-start.6 = (f32[128,512]{1,0:T(8,128)S(1)}, f32[128,512]{1,0:T(8,128)S(1)}, u32[]{:S(2)}, u32[]{:S(2)}) collective-permute-start(f32[128,512]{1,0:T(8,128)S(1)} %fusion.45), channel_id=1, source_target_pairs={{0,4},{4,8},{8,12},{12,16},{16,20},{20,24},{24,28},{1,5},{5,9},{9,... | collective-permute-start | bytes 786440 | tf_op jit(solution)/shard_map/ppermute | solution.py:12
  89.3 1.9 %collective-permute-start.11 = (f32[128,512]{1,0:T(8,128)S(1)}, f32[128,512]{1,0:T(8,128)}, u32[]{:S(2)}, u32[]{:S(2)}) collective-permute-start(f32[128,512]{1,0:T(8,128)S(1)} %collective-permute-done.10), channel_id=1, source_target_pairs={{0,4},{4,8},{8,12},{12,16},{16,20},{20,24},{24,28},{1,5},{5,9},{9,... | collective-permute-start | bytes 786440 | tf_op jit(solution)/shard_map/ppermute | solution.py:12
  91.2 4.7 %collective-permute-done.6 = f32[128,512]{1,0:T(8,128)S(1)} collective-permute-done((f32[128,512]{1,0:T(8,128)S(1)}, f32[128,512]{1,0:T(8,128)S(1)}, u32[]{:S(2)}, u32[]{:S(2)}) %collective-permute-start.6) | collective-permute-done | bytes 262176 | tf_op jit(solution)/shard_map/ppermute | solution.py:12
  96.0 1.3 fusion.44
  97.4 1.9 %collective-permute-start.7 = (f32[128,512]{1,0:T(8,128)S(1)}, f32[128,512]{1,0:T(8,128)S(1)}, u32[]{:S(2)}, u32[]{:S(2)}) collective-permute-start(f32[128,512]{1,0:T(8,128)S(1)} %fusion.44), channel_id=1, source_target_pairs={{0,4},{4,8},{8,12},{12,16},{16,20},{20,24},{24,28},{1,5},{5,9},{9,... | collective-permute-start | bytes 786440 | tf_op jit(solution)/shard_map/ppermute | solution.py:12
  99.3 2.1 %collective-permute-start.12 = (f32[128,512]{1,0:T(8,128)}, f32[128,512]{1,0:T(8,128)S(1)}, u32[]{:S(2)}, u32[]{:S(2)}) collective-permute-start(f32[128,512]{1,0:T(8,128)} %collective-permute-done.11), channel_id=1, source_target_pairs={{0,4},{4,8},{8,12},{12,16},{16,20},{20,24},{24,28},{1,5},{5,9},{9,... | collective-permute-start | bytes 786440 | tf_op jit(solution)/shard_map/ppermute | solution.py:12
  101.4 4.6 %collective-permute-done.7 = f32[128,512]{1,0:T(8,128)S(1)} collective-permute-done((f32[128,512]{1,0:T(8,128)S(1)}, f32[128,512]{1,0:T(8,128)S(1)}, u32[]{:S(2)}, u32[]{:S(2)}) %collective-permute-start.7) | collective-permute-done | bytes 262176 | tf_op jit(solution)/shard_map/ppermute | solution.py:12
  105.9 1.3 fusion.43
  107.3 1.4 collective-permute-start.8
  108.7 0.2 collective-permute-done.12
  108.9 6.8 %collective-permute-done.8 = f32[128,512]{1,0:T(8,128)S(1)} collective-permute-done((f32[128,512]{1,0:T(8,128)S(1)}, f32[128,512]{1,0:T(8,128)S(1)}, u32[]{:S(2)}, u32[]{:S(2)}) %collective-permute-start.8) | collective-permute-done | bytes 262176 | tf_op jit(solution)/shard_map/while/body/eval_jaxpr/ppermute | solution.py:12
  115.8 1.3 fusion.42
  117.1 1.9 %collective-permute-start.13 = (f32[128,512]{1,0:T(8,128)S(1)}, f32[128,512]{1,0:T(8,128)S(1)}, u32[]{:S(2)}, u32[]{:S(2)}) collective-permute-start(f32[128,512]{1,0:T(8,128)S(1)} %fusion.42), channel_id=1, source_target_pairs={{0,4},{4,8},{8,12},{12,16},{16,20},{20,24},{24,28},{1,5},{5,9},{9,... | collective-permute-start | bytes 786440 | tf_op jit(solution)/shard_map/ppermute | solution.py:12
  119.0 6.7 %collective-permute-done.13 = f32[128,512]{1,0:T(8,128)S(1)} collective-permute-done((f32[128,512]{1,0:T(8,128)S(1)}, f32[128,512]{1,0:T(8,128)S(1)}, u32[]{:S(2)}, u32[]{:S(2)}) %collective-permute-start.13) | collective-permute-done | bytes 262176 | tf_op jit(solution)/shard_map/ppermute | solution.py:12
  125.8 1.3 fusion.41
  127.1 1.9 %collective-permute-start.14 = (f32[128,512]{1,0:T(8,128)S(1)}, f32[128,512]{1,0:T(8,128)S(1)}, u32[]{:S(2)}, u32[]{:S(2)}) collective-permute-start(f32[128,512]{1,0:T(8,128)S(1)} %fusion.41), channel_id=1, source_target_pairs={{0,4},{4,8},{8,12},{12,16},{16,20},{20,24},{24,28},{1,5},{5,9},{9,... | collective-permute-start | bytes 786440 | tf_op jit(solution)/shard_map/ppermute | solution.py:12
  129.0 6.7 %collective-permute-done.14 = f32[128,512]{1,0:T(8,128)S(1)} collective-permute-done((f32[128,512]{1,0:T(8,128)S(1)}, f32[128,512]{1,0:T(8,128)S(1)}, u32[]{:S(2)}, u32[]{:S(2)}) %collective-permute-start.14) | collective-permute-done | bytes 262176 | tf_op jit(solution)/shard_map/ppermute | solution.py:12
  135.7 1.3 fusion.40
  137.0 2.1 %collective-permute-start.15 = (f32[128,512]{1,0:T(8,128)S(1)}, f32[128,512]{1,0:T(8,128)S(1)}, u32[]{:S(2)}, u32[]{:S(2)}) collective-permute-start(f32[128,512]{1,0:T(8,128)S(1)} %fusion.40), channel_id=1, source_target_pairs={{0,4},{4,8},{8,12},{12,16},{16,20},{20,24},{24,28},{1,5},{5,9},{9,... | collective-permute-start | bytes 786440 | tf_op jit(solution)/shard_map/ppermute | solution.py:12
  139.1 6.5 %collective-permute-done.15 = f32[128,512]{1,0:T(8,128)S(1)} collective-permute-done((f32[128,512]{1,0:T(8,128)S(1)}, f32[128,512]{1,0:T(8,128)S(1)}, u32[]{:S(2)}, u32[]{:S(2)}) %collective-permute-start.15) | collective-permute-done | bytes 262176 | tf_op jit(solution)/shard_map/ppermute | solution.py:12
  145.7 0.7 copy.44
  146.4 0.9 convert_element_type.105
  147.3 0.4 select_n.199
  147.6 0.3 copy.47
  148.0 1.5 copy.45
  149.5 1.6 fusion.11
  151.1 1.6 fusion.8
  152.7 1.6 fusion.5
  154.3 0.1 convert_bitcast_fusion
  154.4 1.6 fusion.24
  156.1 0.3 pad_maximum_fusion
  156.3 2.4 %copy.51 = bf16[4,512,512]{2,1,0:T(8,128)(2,1)} copy(bf16[4,512,512]{1,2,0:T(8,128)(2,1)S(1)} %pad_maximum_fusion) | data formatting | bytes 4194304 | tf_op jit(solution)/shard_map/stack | solution.py:88
  (38 shorter events, 1.0 us)
Async XLA Ops:
  0.0 47.1 %copy-start.9 = (bf16[4,128,512]{2,1,0:T(8,128)(2,1)S(1)}, bf16[4,128,512]{2,1,0:T(8,128)(2,1)}, u32[]{:S(2)}) copy-start(bf16[4,128,512]{2,1,0:T(8,128)(2,1)} %param.3) | copy-start | bytes 1572868
  0.0 15.8 %collective-permute-start = (bf16[4,128,512]{2,1,0:T(8,128)(2,1)}, bf16[4,128,512]{2,1,0:T(8,128)(2,1)S(1)}, u32[]{:S(2)}, u32[]{:S(2)}) collective-permute-start(bf16[4,128,512]{2,1,0:T(8,128)(2,1)} %param.3), channel_id=1, source_target_pairs={{0,1},{1,2},{2,3},{3,0},{4,5},{5,6},{6,7},{7,4},{8,9},{9,10},{10,1... | collective-permute-start | bytes 1572872 | tf_op jit(solution)/shard_map/ppermute | solution.py:43
  15.8 14.8 %collective-permute-start.1 = (bf16[4,128,512]{2,1,0:T(8,128)(2,1)S(1)}, bf16[4,128,512]{2,1,0:T(8,128)(2,1)}, u32[]{:S(2)}, u32[]{:S(2)}) collective-permute-start(bf16[4,128,512]{2,1,0:T(8,128)(2,1)S(1)} %collective-permute-done), channel_id=1, source_target_pairs={{0,1},{1,2},{2,3},{3,0},{4,5},{5,6},{6,7},{7,4},{8,9},{9,10},{10,1... | collective-permute-start | bytes 1572872 | tf_op jit(solution)/shard_map/ppermute | solution.py:43
  30.7 14.2 %collective-permute-start.2 = (bf16[4,128,512]{2,1,0:T(8,128)(2,1)}, bf16[4,128,512]{2,1,0:T(8,128)(2,1)}, u32[]{:S(2)}, u32[]{:S(2)}) collective-permute-start(bf16[4,128,512]{2,1,0:T(8,128)(2,1)} %collective-permute-done.1), channel_id=1, source_target_pairs={{0,1},{1,2},{2,3},{3,0},{4,5},{5,6},{6,7},{7,4},{8,9},{9,10},{10,1... | collective-permute-start | bytes 1572872 | tf_op jit(solution)/shard_map/ppermute | solution.py:43
  33.1 16.3 %copy-start.1 = (f32[1,512,512]{2,1,0:T(8,128)S(1)}, f32[1,512,512]{2,1,0:T(8,128)}, u32[]{:S(2)}) copy-start(f32[1,512,512]{2,1,0:T(8,128)} %param.5) | copy-start | bytes 3145732
  49.4 2.0 %copy-start = (bf16[4,1024,512]{2,1,0:T(8,128)(2,1)}, bf16[4,1024,512]{2,1,0:T(8,128)(2,1)S(1)}, u32[]{:S(2)}) copy-start(bf16[4,1024,512]{2,1,0:T(8,128)(2,1)S(1)} %constant_dynamic-update-slice_fusion) | copy-start | bytes 12582916
  52.0 17.1 %collective-permute-start.4 = (f32[512,512]{0,1:T(8,128)S(1)}, f32[512,512]{0,1:T(8,128)}, u32[]{:S(2)}, u32[]{:S(2)}) collective-permute-start(f32[512,512]{0,1:T(8,128)S(1)} %fusion.15), channel_id=1, source_target_pairs={{0,4},{4,8},{8,12},{12,16},{16,20},{20,24},{24,28},{1,5},{5,9},{9,... | collective-permute-start | bytes 3145736 | tf_op jit(solution)/shard_map/ppermute | solution.py:12
  56.7 18.1 %collective-permute-start.3 = (f32[128,512]{1,0:T(8,128)}, f32[128,512]{1,0:T(8,128)}, u32[]{:S(2)}, u32[]{:S(2)}) collective-permute-start(f32[128,512]{1,0:T(8,128)} %get-tuple-element.33), channel_id=1, source_target_pairs={{0,4},{4,8},{8,12},{12,16},{16,20},{20,24},{24,28},{1,5},{5,9},{9,... | collective-permute-start | bytes 786440 | tf_op jit(solution)/shard_map/ppermute | solution.py:12
  60.7 18.6 %collective-permute-start.9 = (f32[128,512]{1,0:T(8,128)}, f32[128,512]{1,0:T(8,128)}, u32[]{:S(2)}, u32[]{:S(2)}) collective-permute-start(f32[128,512]{1,0:T(8,128)} %get-tuple-element.32), channel_id=1, source_target_pairs={{0,4},{4,8},{8,12},{12,16},{16,20},{20,24},{24,28},{1,5},{5,9},{9,... | collective-permute-start | bytes 786440 | tf_op jit(solution)/shard_map/ppermute | solution.py:12
  74.8 22.6 %copy-start.2 = (f32[128,1,512]{2,1,0:T(1,128)}, f32[128,1,512]{2,1,0:T(1,128)S(1)}, u32[]{:S(2)}) copy-start(f32[128,1,512]{2,1,0:T(1,128)S(1)} %get-tuple-element.20) | copy-start | bytes 786436
  74.8 22.6 %copy-start.4 = (f32[128,1,512]{2,1,0:T(1,128)}, f32[128,1,512]{2,1,0:T(1,128)S(1)}, u32[]{:S(2)}) copy-start(f32[128,1,512]{2,1,0:T(1,128)S(1)} %get-tuple-element.28) | copy-start | bytes 786436
  74.8 22.6 %copy-start.6 = (f32[128,1,512]{2,1,0:T(1,128)}, f32[128,1,512]{2,1,0:T(1,128)S(1)}, u32[]{:S(2)}) copy-start(f32[128,1,512]{2,1,0:T(1,128)S(1)} %get-tuple-element.30) | copy-start | bytes 786436
  74.8 31.2 %copy-start.8 = (f32[128,1,512]{2,1,0:T(1,128)S(1)}, f32[128,1,512]{2,1,0:T(1,128)}, u32[]{:S(2)}) copy-start(f32[128,1,512]{2,1,0:T(1,128)} %get-tuple-element.19) | copy-start | bytes 786436
  77.4 8.6 %collective-permute-start.5 = (f32[128,512]{1,0:T(8,128)S(1)}, f32[128,512]{1,0:T(8,128)S(1)}, u32[]{:S(2)}, u32[]{:S(2)}) collective-permute-start(f32[128,512]{1,0:T(8,128)S(1)} %fusion.46), channel_id=1, source_target_pairs={{0,4},{4,8},{8,12},{12,16},{16,20},{20,24},{24,28},{1,5},{5,9},{9,... | collective-permute-start | bytes 786440 | tf_op jit(solution)/shard_map/ppermute | solution.py:12
  79.3 10.0 %collective-permute-start.10 = (f32[128,512]{1,0:T(8,128)}, f32[128,512]{1,0:T(8,128)S(1)}, u32[]{:S(2)}, u32[]{:S(2)}) collective-permute-start(f32[128,512]{1,0:T(8,128)} %collective-permute-done.9), channel_id=1, source_target_pairs={{0,4},{4,8},{8,12},{12,16},{16,20},{20,24},{24,28},{1,5},{5,9},{9,... | collective-permute-start | bytes 786440 | tf_op jit(solution)/shard_map/ppermute | solution.py:12
  87.4 8.6 %collective-permute-start.6 = (f32[128,512]{1,0:T(8,128)S(1)}, f32[128,512]{1,0:T(8,128)S(1)}, u32[]{:S(2)}, u32[]{:S(2)}) collective-permute-start(f32[128,512]{1,0:T(8,128)S(1)} %fusion.45), channel_id=1, source_target_pairs={{0,4},{4,8},{8,12},{12,16},{16,20},{20,24},{24,28},{1,5},{5,9},{9,... | collective-permute-start | bytes 786440 | tf_op jit(solution)/shard_map/ppermute | solution.py:12
  89.3 10.0 %collective-permute-start.11 = (f32[128,512]{1,0:T(8,128)S(1)}, f32[128,512]{1,0:T(8,128)}, u32[]{:S(2)}, u32[]{:S(2)}) collective-permute-start(f32[128,512]{1,0:T(8,128)S(1)} %collective-permute-done.10), channel_id=1, source_target_pairs={{0,4},{4,8},{8,12},{12,16},{16,20},{20,24},{24,28},{1,5},{5,9},{9,... | collective-permute-start | bytes 786440 | tf_op jit(solution)/shard_map/ppermute | solution.py:12
  97.4 8.6 %collective-permute-start.7 = (f32[128,512]{1,0:T(8,128)S(1)}, f32[128,512]{1,0:T(8,128)S(1)}, u32[]{:S(2)}, u32[]{:S(2)}) collective-permute-start(f32[128,512]{1,0:T(8,128)S(1)} %fusion.44), channel_id=1, source_target_pairs={{0,4},{4,8},{8,12},{12,16},{16,20},{20,24},{24,28},{1,5},{5,9},{9,... | collective-permute-start | bytes 786440 | tf_op jit(solution)/shard_map/ppermute | solution.py:12
  99.3 26.4 %copy-start.7 = (f32[128,1,512]{2,1,0:T(1,128)S(1)}, f32[128,1,512]{2,1,0:T(1,128)}, u32[]{:S(2)}) copy-start(f32[128,1,512]{2,1,0:T(1,128)} %copy-done.6) | copy-start | bytes 786436
  99.3 36.4 %copy-start.5 = (f32[128,1,512]{2,1,0:T(1,128)S(1)}, f32[128,1,512]{2,1,0:T(1,128)}, u32[]{:S(2)}) copy-start(f32[128,1,512]{2,1,0:T(1,128)} %copy-done.4) | copy-start | bytes 786436
  99.3 9.5 %collective-permute-start.12 = (f32[128,512]{1,0:T(8,128)}, f32[128,512]{1,0:T(8,128)S(1)}, u32[]{:S(2)}, u32[]{:S(2)}) collective-permute-start(f32[128,512]{1,0:T(8,128)} %collective-permute-done.11), channel_id=1, source_target_pairs={{0,4},{4,8},{8,12},{12,16},{16,20},{20,24},{24,28},{1,5},{5,9},{9,... | collective-permute-start | bytes 786440 | tf_op jit(solution)/shard_map/ppermute | solution.py:12
  107.2 38.4 %copy-start.3 = (f32[128,1,512]{2,1,0:T(1,128)S(1)}, f32[128,1,512]{2,1,0:T(1,128)}, u32[]{:S(2)}) copy-start(f32[128,1,512]{2,1,0:T(1,128)} %copy-done.2) | copy-start | bytes 786436
  107.3 8.4 %collective-permute-start.8 = (f32[128,512]{1,0:T(8,128)S(1)}, f32[128,512]{1,0:T(8,128)S(1)}, u32[]{:S(2)}, u32[]{:S(2)}) collective-permute-start(f32[128,512]{1,0:T(8,128)S(1)} %fusion.43), channel_id=1, source_target_pairs={{0,16},{4,20},{8,24},{12,28},{1,17},{5,21},{9,25},{13,29},{2,18},{... | collective-permute-start | bytes 786440 | tf_op jit(solution)/shard_map/while/body/eval_jaxpr/ppermute | solution.py:12
  117.1 8.6 %collective-permute-start.13 = (f32[128,512]{1,0:T(8,128)S(1)}, f32[128,512]{1,0:T(8,128)S(1)}, u32[]{:S(2)}, u32[]{:S(2)}) collective-permute-start(f32[128,512]{1,0:T(8,128)S(1)} %fusion.42), channel_id=1, source_target_pairs={{0,4},{4,8},{8,12},{12,16},{16,20},{20,24},{24,28},{1,5},{5,9},{9,... | collective-permute-start | bytes 786440 | tf_op jit(solution)/shard_map/ppermute | solution.py:12
  127.1 8.6 %collective-permute-start.14 = (f32[128,512]{1,0:T(8,128)S(1)}, f32[128,512]{1,0:T(8,128)S(1)}, u32[]{:S(2)}, u32[]{:S(2)}) collective-permute-start(f32[128,512]{1,0:T(8,128)S(1)} %fusion.41), channel_id=1, source_target_pairs={{0,4},{4,8},{8,12},{12,16},{16,20},{20,24},{24,28},{1,5},{5,9},{9,... | collective-permute-start | bytes 786440 | tf_op jit(solution)/shard_map/ppermute | solution.py:12
  137.0 8.6 %collective-permute-start.15 = (f32[128,512]{1,0:T(8,128)S(1)}, f32[128,512]{1,0:T(8,128)S(1)}, u32[]{:S(2)}, u32[]{:S(2)}) collective-permute-start(f32[128,512]{1,0:T(8,128)S(1)} %fusion.40), channel_id=1, source_target_pairs={{0,4},{4,8},{8,12},{12,16},{16,20},{20,24},{24,28},{1,5},{5,9},{9,... | collective-permute-start | bytes 786440 | tf_op jit(solution)/shard_map/ppermute | solution.py:12
